TPU v7x, 256 devices: a 8x8x2 block of a 8x8x16 slice. The times are simulated.
256 devices in a mesh: win: 2 (over z), trow: 128 (over y, x, core).
Axes of the slice: x: 8, y: 8, z: 2, core: 2. Of those that a mesh axis runs over, the one named last changes fastest.
The devices are a block of a 8x8x16 slice.
Arguments:
- coverage: int32 [65536, 2048], P(('win', 'trow')), parts along dimension 0, may hold values from 0 to 1, as said below
- dose_level: float32 [65536, 2048], P(('win', 'trow')), parts along dimension 0, may hold values from 0.5 to 2
Outputs:
- dosage: float32 [65536, 2048], P(('win', 'trow')), parts along dimension 0
- exposure: float32 [65536, 2048], P(('win', 'trow')), parts along dimension 0
There are 2 independent parts, one for each index of `win`. A program takes and returns all parts, laid end to end along the dimension named above; each array names one. Nothing has to cross between parts.
Inputs may be any that keep to these rules, and one draw needn't show every extreme that they name: Every aligned 512 x 512 block of pixels holds at least one pixel with coverage 1.
All inputs are finite; a program needn't handle non-finite values.
Results may differ from a plain program's by a relative error of at most 0.00018.
Values sent between devices are 32-bit elements; how exact they have to be, the bound alone decides.
A program may use at most 64 MiB of HBM per device.

v0:
```python
import math

import jax
import jax.numpy as jnp
from jax import lax
from jax.sharding import PartitionSpec as P

R = 128
BLOCK = 128
F = 512
SIG_FWD = 5
SIG_MID = 50
SIG_BACK = 3000
OUTER = 2
INNER = 2


highest = lax.Precision.HIGHEST
backscatter_ratio = 0.7


def over_pieces(shard, axis):
    return lax.all_gather(shard, axis).sum(0)


def with_halo(shard, sides, width):
    for axis, dim in sides:
        devices, length = (lax.axis_size(axis), shard.shape[dim])
        up = [(i, (i + 1) % devices) for i in range(devices - 1)]
        down = [(j, i) for i, j in up]
        last = lax.slice_in_dim(shard, length - width, length, axis=dim)
        leading = lax.slice_in_dim(shard, 0, width, axis=dim)
        before = lax.ppermute(last, axis, up)
        after = lax.ppermute(leading, axis, down)
        shard = jnp.concatenate([before, shard, after], axis=dim)
    return shard


def raw_profile(offset):
    first = 0.5 * jnp.exp(-offset * offset / (2.0 * SIG_FWD**2)) / SIG_FWD
    second = 0.5 * jnp.exp(-offset * offset / (2.0 * SIG_MID**2)) / SIG_MID
    return first + second


def short_weight(offset):
    support = jnp.arange(-R, R + 1, dtype=jnp.float32)
    normal = jnp.sum(raw_profile(support))
    return jnp.where(jnp.abs(offset) <= R, raw_profile(offset) / normal, 0.0)


def back_weight(offset):
    spacing = offset * F
    return (
        F
        * jnp.exp(-spacing * spacing / (2.0 * SIG_BACK**2))
        / (math.sqrt(2.0 * math.pi) * SIG_BACK)
    )


def smooth_columns(field):
    leading = field.shape[:-1]
    count = field.shape[-1] // BLOCK
    blocked = field.reshape(leading + (count, BLOCK))
    zero_block = jnp.zeros(leading + (1, BLOCK), field.dtype)
    before = jnp.concatenate([zero_block, blocked[..., :-1, :]], axis=-2)
    after = jnp.concatenate([blocked[..., 1:, :], zero_block], axis=-2)
    framed = jnp.concatenate([before, blocked, after], axis=-1)
    inner_index = jnp.arange(BLOCK + 2 * R, dtype=jnp.float32)[:, None]
    outer_index = jnp.arange(BLOCK, dtype=jnp.float32)[None, :]
    matrix = short_weight(inner_index - R - outer_index)
    result = jnp.einsum("...bp,pq->...bq", framed, matrix, precision=highest)
    return result.reshape(field.shape)


def band_matrix(out_rows, margin):
    out_index = jnp.arange(out_rows, dtype=jnp.float32)[:, None]
    in_index = jnp.arange(out_rows + 2 * margin, dtype=jnp.float32)[None, :]
    return short_weight(in_index - margin - out_index)


def vertical_product(matrix, padded, own, margin):
    count = own.shape[0]
    inside = jnp.dot(matrix[:, margin : margin + count], own, precision=highest)
    above = jnp.dot(matrix[:, :margin], padded[:margin], precision=highest)
    below = jnp.dot(matrix[:, margin + count :], padded[margin + count :], precision=highest)
    return inside + above + below


def spread_rows(backscatter, first_row, count):
    coarse_count, coarse_width = backscatter.shape
    coarse_index = (first_row + jnp.arange(count, dtype=jnp.int32)) // F
    selector = (coarse_index[:, None] == jnp.arange(coarse_count, dtype=jnp.int32)[None, :]).astype(
        jnp.float32
    )
    rowwise = jnp.dot(selector, backscatter, precision=highest)
    return jnp.broadcast_to(rowwise[:, :, None], (count, coarse_width, F)).reshape(
        count, coarse_width * F
    )


def per_device(coverage, dose_level):
    rows_here, width = coverage.shape
    devices = lax.axis_size("trow")
    coarse_count = rows_here * devices // F
    coarse_width = width // F
    first_row = lax.axis_index("trow") * rows_here
    target = jnp.where(coverage == 1, dose_level, 0.0)
    dosage = target
    row_ids = jnp.arange(coarse_count, dtype=jnp.float32)
    col_ids = jnp.arange(coarse_width, dtype=jnp.float32)
    vertical_kernel = back_weight(row_ids[:, None] - row_ids[None, :])
    lateral_kernel = back_weight(col_ids[:, None] - col_ids[None, :])
    group = min(rows_here, F)
    local_blocks = rows_here // group
    cell_ids = jnp.arange(coarse_count, dtype=jnp.int32)
    block_starts = first_row + jnp.arange(local_blocks, dtype=jnp.int32) * group
    owner = (cell_ids[:, None] == (block_starts // F)[None, :]).astype(jnp.float32)
    short_matrix = band_matrix(rows_here, R)
    exposure = dosage
    for outer_step in range(OUTER):
        pieces = dosage.reshape(local_blocks, group, coarse_width, F).sum(axis=(1, 3))
        partial_value = jnp.dot(owner, pieces, precision=highest)
        sums = over_pieces(partial_value, "trow")
        coarse = sums / (F * F)
        lateral = jnp.dot(coarse, lateral_kernel, precision=highest)
        backscatter = jnp.dot(vertical_kernel, lateral, precision=highest)
        spread_own = spread_rows(backscatter, first_row, rows_here)
        for inner_step in range(INNER):
            padded = with_halo(dosage, (("trow", 0),), R)
            vertical = vertical_product(short_matrix, padded, dosage, R)
            exposure = smooth_columns(vertical) + backscatter_ratio * spread_own
            dosage = dosage * target / exposure
    return (dosage, exposure)


def solution(mesh):
    return jax.shard_map(
        per_device,
        mesh=mesh,
        in_specs=(P(("win", "trow"), None), P(("win", "trow"), None)),
        out_specs=(P(("win", "trow"), None), P(("win", "trow"), None)),
        check_vma=False,
    )
```

profile of v0, /device:TPU:513, one launch (start us, length us, event | category | flops | bytes accessed | tf_op | source)
XLA Modules:
  0.0 277.2 jit_solution(9056512776589124183)
XLA Ops:
  0.6 2.7 fusion.135
  3.3 1.5 fusion.143
  4.9 22.3 %collective-permute-start.1 = (f32[128,2048]{1,0:T(8,128)}, f32[128,2048]{1,0:T(8,128)}, u32[]{:S(2)}, u32[]{:S(2)}) collective-permute-start(f32[128,2048]{1,0:T(8,128)} %get-tuple-element.22), channel_id=1, source_target_pairs={{1,0},{2,1},{3,2},{4,3},{5,4},{6,5},{7,6},{8,7},{9,8},{10,9},{11,1... | collective-permute-start | bytes 3145736 | tf_op jit(solution)/shard_map/ppermute | solution.py:34
  27.2 2.0 collective-permute-start
  29.4 48.3 %all-gather.2 = f32[128,64,4]{1,2,0:T(4,128)S(1)} all-gather(f32[1,64,4]{1,2,0:T(4,128)S(1)} %multiply_bitcast_fusion.1), channel_id=2, replica_groups=mesh['win'=2,'trow'=128] {'trow'}, dimensions={0}, use_global_device_ids=true | all-gather | bytes 132096 | tf_op jit(solution)/shard_map/all_gather | solution.py:23
  77.9 0.2 fusion.72
  78.1 0.2 fusion.59
  78.3 0.2 convolution_multiply_fusion.1
  78.7 0.3 broadcast_in_dim.22
  79.1 2.2 copy.80
  81.3 1.1 add_reduce_fusion
  82.4 0.9 divide_select_fusion
  83.4 1.9 fusion.38
  85.3 3.0 %convolution_add_fusion.7 = f32[256,2048]{1,0:T(8,128)S(1)} fusion(f32[256,2048]{1,0:T(8,128)S(1)} %fusion.38, f32[128,2048]{1,0:T(8,128)} %collective-permute-done, f32[256,512]{1,0:T(8,128)S(1)} %divide_select_fusion), kind=kOutput, calls=%fused_computation.45 | convolution fusion | flops 805830656 | bytes 5373952 | tf_op jit(solution)/shard_map/dot_general | solution.py:84
  88.4 3.0 %fusion.28 = f32[32,16,8,128]{3,2,1,0:T(8,128)S(1)} fusion(f32[256,2048]{1,0:T(8,128)S(1)} %convolution_add_fusion.7, f32[128,2048]{1,0:T(8,128)} %collective-permute-done.1, f32[256,512]{1,0:T(8,128)S(1)} %divide_select_fusion), kind=kOutput, calls=%fused_computation.55 | convolution fusion | flops 805830656 | bytes 5373952 | tf_op jit(solution)/shard_map/dot_general | solution.py:85
  91.4 0.2 copy.89
  91.6 0.4 fusion.142
  92.1 8.7 %fusion.9 = f32[256,16,128]{0,2,1:T(8,128)} fusion(f32[256,15,128]{2,0,1:T(8,128)S(1)} %get-tuple-element.21, f32[256,15,128]{2,0,1:T(8,128)S(1)} %get-tuple-element.20, f32[256,16,128]{2,0,1:T(8,128)S(1)} %bitcast.66, f32[]{:T(128)} %add_reduce_fusion, f32[384]{0:T(512)S(1)} %iota_add_fusion), kind=kOutput, calls=%fused_computation.16 | convolution fusion | flops 2425946112 | bytes 8128004 | tf_op jit(solution)/shard_map/...bp,pq->...bq/dot_general | solution.py:71
  100.8 2.9 %copy.62 = f32[256,2048]{1,0:T(8,128)} copy(f32[256,2048]{0,1:T(8,128)} %bitcast.74) | data formatting | bytes 4194304 | tf_op jit(solution)/shard_map/reshape | solution.py:72
  103.7 2.8 %add_divide_fusion.2 = f32[256,2048]{1,0:T(8,128)S(1)} fusion(f32[256,2048]{1,0:T(8,128)} %copy.62, f32[256,2048]{1,0:T(8,128)} %bitcast.61, f32[256,2048]{1,0:T(8,128)S(1)} %get-tuple-element.7), kind=kLoop, calls=%fused_computation.53 | loop fusion | flops 1572864 | bytes 8388608 | tf_op jit(solution)/shard_map/div | solution.py:132
  106.6 3.6 %collective-permute-start.2 = (f32[128,2048]{1,0:T(8,128)S(1)}, f32[128,2048]{1,0:T(8,128)S(1)}, u32[]{:S(2)}, u32[]{:S(2)}) collective-permute-start(f32[128,2048]{1,0:T(8,128)S(1)} %get-tuple-element.19), channel_id=1, source_target_pairs={{0,1},{1,2},{2,3},{3,4},{4,5},{5,6},{6,7},{7,8},{8,9},{9,10},{10,1... | collective-permute-start | bytes 3145736 | tf_op jit(solution)/shard_map/ppermute | solution.py:33
  110.2 2.1 collective-permute-start.3
  112.3 1.9 fusion.36
  114.2 7.7 %collective-permute-done.2 = f32[128,2048]{1,0:T(8,128)S(1)} collective-permute-done((f32[128,2048]{1,0:T(8,128)S(1)}, f32[128,2048]{1,0:T(8,128)S(1)}, u32[]{:S(2)}, u32[]{:S(2)}) %collective-permute-start.2) | collective-permute-done | bytes 1048608 | tf_op jit(solution)/shard_map/ppermute | solution.py:33
  121.9 1.8 convolution_add_fusion.5
  123.7 2.6 collective-permute-done.3
  126.3 1.8 fusion.29
  128.1 0.2 copy.88
  128.4 0.4 fusion.140
  128.8 8.7 %fusion.6 = f32[256,16,128]{0,2,1:T(8,128)} fusion(f32[256,15,128]{2,0,1:T(8,128)S(1)} %get-tuple-element.17, f32[256,15,128]{2,0,1:T(8,128)S(1)} %get-tuple-element.16, f32[256,16,128]{2,0,1:T(8,128)S(1)} %bitcast.68, f32[]{:T(128)} %add_reduce_fusion, f32[384]{0:T(512)S(1)} %iota_add_fusion), kind=kOutput, calls=%fused_computation.11 | convolution fusion | flops 2425946112 | bytes 8128004 | tf_op jit(solution)/shard_map/...bp,pq->...bq/dot_general | solution.py:71
  137.5 2.9 %copy.66 = f32[256,2048]{1,0:T(8,128)} copy(f32[256,2048]{0,1:T(8,128)} %bitcast.75) | data formatting | bytes 4194304 | tf_op jit(solution)/shard_map/reshape | solution.py:72
  140.4 5.2 %fusion.134 = (f32[2048]{0:T(1024)S(1)}, f32[256,2048]{1,0:T(8,128)}) fusion(f32[256,2048]{1,0:T(8,128)} %copy.66, f32[256,2048]{1,0:T(8,128)} %bitcast.62, f32[256,2048]{1,0:T(8,128)} %copy-done.2, f32[256,2048]{1,0:T(8,128)S(1)} %get-tuple-element.7), kind=kLoop, calls=%fused_computation.179 | loop fusion | flops 2095104 | bytes 10493952 | tf_op jit(solution)/shard_map/reduce_sum | solution.py:121
  145.7 3.1 %fusion.139 = (f32[128,2048]{1,0:T(8,128)}, f32[128,2048]{1,0:T(8,128)}) fusion(f32[256,2048]{1,0:T(8,128)} %get-tuple-element.5), kind=kLoop, calls=%fused_computation.184 | loop fusion | bytes 4194304 | tf_op jit(solution)/shard_map/slice | solution.py:32
  148.8 1.9 collective-permute-start.4
  150.8 52.0 %all-gather.3 = f32[128,64,4]{1,2,0:T(4,128)S(1)} all-gather(f32[1,64,4]{1,2,0:T(4,128)S(1)} %multiply_bitcast_fusion), channel_id=3, replica_groups=mesh['win'=2,'trow'=128] {'trow'}, dimensions={0}, use_global_device_ids=true | all-gather | bytes 132096 | tf_op jit(solution)/shard_map/all_gather | solution.py:23
  203.0 2.3 collective-permute-start.5
  205.3 0.2 fusion.70
  205.5 0.2 fusion.57
  205.7 0.2 convolution_multiply_fusion
  205.9 0.2 copy.70
  206.1 0.3 broadcast_in_dim.23
  206.4 2.2 copy.81
  208.7 1.9 fusion.34
  210.6 3.0 %convolution_add_fusion.3 = f32[256,2048]{1,0:T(8,128)S(1)} fusion(f32[256,2048]{1,0:T(8,128)S(1)} %fusion.34, f32[128,2048]{1,0:T(8,128)} %collective-permute-done.4, f32[256,512]{1,0:T(8,128)S(1)} %divide_select_fusion), kind=kOutput, calls=%fused_computation.41 | convolution fusion | flops 805830656 | bytes 5373952 | tf_op jit(solution)/shard_map/dot_general | solution.py:84
  213.7 5.7 %collective-permute-done.5 = f32[128,2048]{1,0:T(8,128)} collective-permute-done((f32[128,2048]{1,0:T(8,128)}, f32[128,2048]{1,0:T(8,128)}, u32[]{:S(2)}, u32[]{:S(2)}) %collective-permute-start.5) | collective-permute-done | bytes 1048608 | tf_op jit(solution)/shard_map/ppermute | solution.py:34
  219.4 3.0 %fusion.30 = f32[32,16,8,128]{3,2,1,0:T(8,128)S(1)} fusion(f32[256,2048]{1,0:T(8,128)S(1)} %convolution_add_fusion.3, f32[128,2048]{1,0:T(8,128)} %collective-permute-done.5, f32[256,512]{1,0:T(8,128)S(1)} %divide_select_fusion), kind=kOutput, calls=%fused_computation.57 | convolution fusion | flops 805830656 | bytes 5373952 | tf_op jit(solution)/shard_map/dot_general | solution.py:85
  222.5 0.2 copy.87
  222.7 0.4 fusion.138
  223.1 8.7 %fusion.3 = f32[256,16,128]{0,2,1:T(8,128)} fusion(f32[256,15,128]{2,0,1:T(8,128)S(1)} %get-tuple-element.13, f32[256,15,128]{2,0,1:T(8,128)S(1)} %get-tuple-element.12, f32[256,16,128]{2,0,1:T(8,128)S(1)} %bitcast.70, f32[]{:T(128)} %add_reduce_fusion, f32[384]{0:T(512)S(1)} %iota_add_fusion), kind=kOutput, calls=%fused_computation.6 | convolution fusion | flops 2425946112 | bytes 8128004 | tf_op jit(solution)/shard_map/...bp,pq->...bq/dot_general | solution.py:71
  231.8 2.9 %copy.71 = f32[256,2048]{1,0:T(8,128)} copy(f32[256,2048]{0,1:T(8,128)} %bitcast.76) | data formatting | bytes 4194304 | tf_op jit(solution)/shard_map/reshape | solution.py:72
  234.7 3.6 %add_divide_fusion = f32[256,2048]{1,0:T(8,128)S(1)} fusion(f32[256,2048]{1,0:T(8,128)} %copy.71, f32[256,2048]{1,0:T(8,128)} %bitcast.59, f32[256,2048]{1,0:T(8,128)} %get-tuple-element.5, f32[256,2048]{1,0:T(8,128)S(1)} %get-tuple-element.7), kind=kLoop, calls=%fused_computation.51 | loop fusion | flops 1572864 | bytes 10485760 | tf_op jit(solution)/shard_map/div | solution.py:132
  238.4 0.2 fusion.137
  238.6 2.0 collective-permute-start.6
  240.5 2.8 collective-permute-start.7
  243.3 1.9 fusion.32
  245.2 7.0 %collective-permute-done.6 = f32[128,2048]{1,0:T(8,128)S(1)} collective-permute-done((f32[128,2048]{1,0:T(8,128)S(1)}, f32[128,2048]{1,0:T(8,128)S(1)}, u32[]{:S(2)}, u32[]{:S(2)}) %collective-permute-start.6) | collective-permute-done | bytes 1048608 | tf_op jit(solution)/shard_map/ppermute | solution.py:33
  252.3 1.8 convolution_add_fusion.1
  254.1 2.6 collective-permute-done.7
  256.7 1.8 fusion.31
  258.5 0.2 copy.86
  258.7 0.4 fusion.136
  259.2 8.7 %fusion = f32[256,16,128]{0,2,1:T(8,128)} fusion(f32[256,15,128]{2,0,1:T(8,128)S(1)} %get-tuple-element.9, f32[256,15,128]{2,0,1:T(8,128)S(1)} %get-tuple-element.8, f32[256,16,128]{2,0,1:T(8,128)S(1)} %bitcast.64, f32[]{:T(128)} %add_reduce_fusion, f32[384]{0:T(512)S(1)} %iota_add_fusion), kind=kOutput, calls=%fused_computation.1 | convolution fusion | flops 2425946112 | bytes 8128004 | tf_op jit(solution)/shard_map/...bp,pq->...bq/dot_general | solution.py:71
  267.9 2.9 %copy.75 = f32[256,2048]{1,0:T(8,128)} copy(f32[256,2048]{0,1:T(8,128)} %bitcast.73) | data formatting | bytes 4194304 | tf_op jit(solution)/shard_map/reshape | solution.py:72
  270.8 6.0 %multiply_divide_fusion = (f32[256,2048]{1,0:T(8,128)}, f32[256,2048]{1,0:T(8,128)}) fusion(f32[256,2048]{1,0:T(8,128)} %copy-done.1, f32[256,2048]{1,0:T(8,128)S(1)} %get-tuple-element.7, f32[256,2048]{1,0:T(8,128)} %copy.75, f32[256,2048]{1,0:T(8,128)} %bitcast.60), kind=kLoop, calls=%fused_computation.50 | loop fusion | flops 1572864 | bytes 12582912 | tf_op jit(solution)/shard_map/div | solution.py:132
  (23 shorter events, 1.1 us)
Async XLA Ops:
  4.9 83.5 %collective-permute-start.1 = (f32[128,2048]{1,0:T(8,128)}, f32[128,2048]{1,0:T(8,128)}, u32[]{:S(2)}, u32[]{:S(2)}) collective-permute-start(f32[128,2048]{1,0:T(8,128)} %get-tuple-element.22), channel_id=1, source_target_pairs={{1,0},{2,1},{3,2},{4,3},{5,4},{6,5},{7,6},{8,7},{9,8},{10,9},{11,1... | collective-permute-start | bytes 3145736 | tf_op jit(solution)/shard_map/ppermute | solution.py:34
  27.2 58.1 %collective-permute-start = (f32[128,2048]{1,0:T(8,128)}, f32[128,2048]{1,0:T(8,128)}, u32[]{:S(2)}, u32[]{:S(2)}) collective-permute-start(f32[128,2048]{1,0:T(8,128)} %get-tuple-element.23), channel_id=1, source_target_pairs={{0,1},{1,2},{2,3},{3,4},{4,5},{5,6},{6,7},{7,8},{8,9},{9,10},{10,1... | collective-permute-start | bytes 3145736 | tf_op jit(solution)/shard_map/ppermute | solution.py:33
  106.4 5.9 %copy-start.2 = (f32[256,2048]{1,0:T(8,128)}, f32[256,2048]{1,0:T(8,128)S(1)}, u32[]{:S(2)}) copy-start(f32[256,2048]{1,0:T(8,128)S(1)} %add_divide_fusion.2) | copy-start | bytes 6291460
  106.6 15.3 %collective-permute-start.2 = (f32[128,2048]{1,0:T(8,128)S(1)}, f32[128,2048]{1,0:T(8,128)S(1)}, u32[]{:S(2)}, u32[]{:S(2)}) collective-permute-start(f32[128,2048]{1,0:T(8,128)S(1)} %get-tuple-element.19), channel_id=1, source_target_pairs={{0,1},{1,2},{2,3},{3,4},{4,5},{5,6},{6,7},{7,8},{8,9},{9,10},{10,1... | collective-permute-start | bytes 3145736 | tf_op jit(solution)/shard_map/ppermute | solution.py:33
  110.2 16.1 %collective-permute-start.3 = (f32[128,2048]{1,0:T(8,128)S(1)}, f32[128,2048]{1,0:T(8,128)S(1)}, u32[]{:S(2)}, u32[]{:S(2)}) collective-permute-start(f32[128,2048]{1,0:T(8,128)S(1)} %get-tuple-element.18), channel_id=1, source_target_pairs={{1,0},{2,1},{3,2},{4,3},{5,4},{6,5},{7,6},{8,7},{9,8},{10,9},{11,1... | collective-permute-start | bytes 3145736 | tf_op jit(solution)/shard_map/ppermute | solution.py:34
  148.8 61.8 %collective-permute-start.4 = (f32[128,2048]{1,0:T(8,128)}, f32[128,2048]{1,0:T(8,128)}, u32[]{:S(2)}, u32[]{:S(2)}) collective-permute-start(f32[128,2048]{1,0:T(8,128)} %get-tuple-element.15), channel_id=1, source_target_pairs={{0,1},{1,2},{2,3},{3,4},{4,5},{5,6},{6,7},{7,8},{8,9},{9,10},{10,1... | collective-permute-start | bytes 3145736 | tf_op jit(solution)/shard_map/ppermute | solution.py:33
  203.0 16.5 %collective-permute-start.5 = (f32[128,2048]{1,0:T(8,128)}, f32[128,2048]{1,0:T(8,128)}, u32[]{:S(2)}, u32[]{:S(2)}) collective-permute-start(f32[128,2048]{1,0:T(8,128)} %get-tuple-element.14), channel_id=1, source_target_pairs={{1,0},{2,1},{3,2},{4,3},{5,4},{6,5},{7,6},{8,7},{9,8},{10,9},{11,1... | collective-permute-start | bytes 3145736 | tf_op jit(solution)/shard_map/ppermute | solution.py:34
  206.4 2.3 copy-start
  238.3 5.0 %copy-start.1 = (f32[256,2048]{1,0:T(8,128)}, f32[256,2048]{1,0:T(8,128)S(1)}, u32[]{:S(2)}) copy-start(f32[256,2048]{1,0:T(8,128)S(1)} %add_divide_fusion) | copy-start | bytes 6291460
  238.6 13.7 %collective-permute-start.6 = (f32[128,2048]{1,0:T(8,128)S(1)}, f32[128,2048]{1,0:T(8,128)S(1)}, u32[]{:S(2)}, u32[]{:S(2)}) collective-permute-start(f32[128,2048]{1,0:T(8,128)S(1)} %get-tuple-element.11), channel_id=1, source_target_pairs={{0,1},{1,2},{2,3},{3,4},{4,5},{5,6},{6,7},{7,8},{8,9},{9,10},{10,1... | collective-permute-start | bytes 3145736 | tf_op jit(solution)/shard_map/ppermute | solution.py:33
  240.5 16.1 %collective-permute-start.7 = (f32[128,2048]{1,0:T(8,128)S(1)}, f32[128,2048]{1,0:T(8,128)S(1)}, u32[]{:S(2)}, u32[]{:S(2)}) collective-permute-start(f32[128,2048]{1,0:T(8,128)S(1)} %get-tuple-element.10), channel_id=1, source_target_pairs={{1,0},{2,1},{3,2},{4,3},{5,4},{6,5},{7,6},{8,7},{9,8},{10,9},{11,1... | collective-permute-start | bytes 3145736 | tf_op jit(solution)/shard_map/ppermute | solution.py:34
where the time goes:
time: 281 us; the launch traced here: 277 us
  blocking collectives  100 us (36%)
  matrix products  63.1 us (22%)
  starting transfers between devices  38.9 us (14%)
  waiting for transfers between devices  25.6 us (9%)
  local copies, waits for them, and re-layouts  24.6 us (9%)
  other arithmetic  23.1 us (8%)
    all_gather x2, blocking collectives, over_pieces(): return lax.all_gather(shard, axis).sum(0)  100 us
    dot_general x4, matrix products, smooth_columns(): result = jnp.einsum('...bp,pq->...bq', framed, matrix, precision=highest)  34.9 us
    ppermute x4, starting transfers between devices, with_halo(): after = lax.ppermute(leading, axis, down)  29.5 us
    ppermute x4, waiting for transfers between devices, with_halo(): before = lax.ppermute(last, axis, up)  14.7 us
    div x3, other arithmetic, per_device(): dosage = dosage * target / exposure  12.4 us
    reshape x4, local copies, waits for them, and re-layouts, smooth_columns(): return result.reshape(field.shape)  11.5 us
    ppermute x4, waiting for transfers between devices, with_halo(): after = lax.ppermute(leading, axis, down)  11 us
    dot_general x4, matrix products, vertical_product(): above = jnp.dot(matrix[:, :margin], padded[:margin], precision=highest)  9.68 us
  transfers between devices with their start and end apart: 8, of which 5 were waited for; matrix products, arithmetic and copies ran while one was open for 10% of the time, Pallas kernels for 0%

commit v1 on v0

v1 whole, which is shorter than its diff:
```python
import functools
import math

import jax
import jax.numpy as jnp
import numpy as np
from jax import lax
from jax.experimental import pallas as pl
from jax.experimental.pallas import tpu as pltpu
from jax.sharding import PartitionSpec as P

R = 128
F = 512
SIG_FWD = 5
SIG_MID = 50
SIG_BACK = 3000
OUTER = 2
INNER = 2
PASSES = OUTER * INNER
CB = 256
LANES = 128
backscatter_ratio = 0.7
MESH = pl.DeviceIdType.MESH


def raw_profile(offset):
    first = 0.5 * np.exp(-offset * offset / (2.0 * SIG_FWD**2)) / SIG_FWD
    second = 0.5 * np.exp(-offset * offset / (2.0 * SIG_MID**2)) / SIG_MID
    return first + second


def short_weight(offset):
    normal = np.sum(raw_profile(np.arange(-R, R + 1, dtype=np.float64)))
    return np.where(np.abs(offset) <= R, raw_profile(offset) / normal, 0.0)


def back_weight(offset):
    spacing = offset * F
    return (
        F
        * np.exp(-spacing * spacing / (2.0 * SIG_BACK**2))
        / (math.sqrt(2.0 * math.pi) * SIG_BACK)
    )


def two_parts(matrix):
    whole = jnp.asarray(matrix, jnp.float32)
    high = whole.astype(jnp.bfloat16)
    low = (whole - high.astype(jnp.float32)).astype(jnp.bfloat16)
    return high, low


def vertical_matrix(rows):
    out = np.arange(rows, dtype=np.float64)[:, None]
    own = np.arange(rows, dtype=np.float64)
    above = np.arange(-R, 0, dtype=np.float64)
    below = np.arange(rows, rows + R, dtype=np.float64)
    return short_weight(out - np.concatenate([own, above, below])[None, :])


def horizontal_matrix():
    inner = np.arange(CB + 2 * R, dtype=np.float64)[:, None]
    outer = np.arange(CB, dtype=np.float64)[None, :]
    return short_weight(inner - R - outer)


def split(value):
    high = value.astype(jnp.bfloat16)
    low = (value - high.astype(jnp.float32)).astype(jnp.bfloat16)
    return high, low


def dot(left, right):
    return jnp.dot(left, right, preferred_element_type=jnp.float32)


def kernel(
    n, nx, ny,
    cov_hbm, dose_hbm, ah_hbm, al_hbm, bh_hbm, bl_hbm, gtab_hbm,
    dout_hbm, eout_hbm,
    cov, dose, ah, al, bh, bl, gtab,
    dbuf, dh, dl, up, down, vh, vl, dout, eout,
    accs, spread, row_out, row_in, yrows, xout, xrows,
    load_sem, const_sem, out_sem,
    up_send, down_send, up_recv, down_recv,
    a_send, a_recv, y_send, y_recv, x_send, x_recv,
):
    height, width = cov.shape
    blocks = width // CB
    cells = width // F
    group = LANES // cells
    me = lax.axis_index("trow")
    chip, core = me // 2, me % 2
    y, x = chip // nx, chip % nx
    partner = me + 1 - 2 * core
    has_up, has_down = me > 0, me < n - 1
    fwd, bwd = nx // 2, (nx - 1) // 2

    def device(yy, xx, cc):
        return (yy * nx + xx) * 2 + cc

    def load(b):
        cols = pl.ds(b * CB, CB)
        return (
            pltpu.make_async_copy(cov_hbm.at[:, cols], cov.at[:, cols], load_sem.at[0, b]),
            pltpu.make_async_copy(dose_hbm.at[:, cols], dose.at[:, cols], load_sem.at[1, b]),
        )

    for b in range(blocks):
        for copy in load(b):
            copy.start()
    consts = [
        pltpu.make_async_copy(source, target, const_sem.at[k])
        for k, (source, target) in enumerate(
            [(ah_hbm, ah), (al_hbm, al), (bh_hbm, bh), (bl_hbm, bl), (gtab_hbm, gtab)]
        )
    ]
    for copy in consts:
        copy.start()

    barrier = pltpu.get_barrier_semaphore()

    def greet(other):
        pl.semaphore_signal(barrier, inc=1, device_id={"trow": other}, device_id_type=MESH)

    @pl.when(has_up)
    def _():
        greet(me - 1)

    @pl.when(has_down)
    def _():
        greet(me + 1)

    for d in range(1, ny):
        greet(device((y + d) % ny, x, core))
    for d in range(1, fwd + 1):
        greet(device(y, (x + nx - d) % nx, 0))
    for d in range(1, bwd + 1):
        greet(device(y, (x + d) % nx, 1))

    zero_pad = jnp.zeros((height, R), jnp.bfloat16)
    for part in (vh, vl):
        part[:, 0:R] = zero_pad
        part[:, R + width : R + width + R] = zero_pad

    @pl.when(me == 0)
    def _():
        up[...] = jnp.zeros_like(up)

    @pl.when(me == n - 1)
    def _():
        down[...] = jnp.zeros_like(down)

    accs[...] = jnp.zeros_like(accs)
    pl.semaphore_wait(
        barrier,
        has_up.astype(jnp.int32)
        + has_down.astype(jnp.int32)
        + (ny - 1)
        + 2 * jnp.where(core == 0, fwd, bwd),
    )

    def up_copy(p, cols, b):
        return pltpu.make_async_remote_copy(
            src_ref=dbuf.at[p, pl.ds(0, R), cols],
            dst_ref=down.at[p, :, cols],
            send_sem=up_send.at[p],
            recv_sem=down_recv.at[p, b],
            device_id={"trow": me - 1},
            device_id_type=MESH,
        )

    def down_copy(p, cols, b):
        return pltpu.make_async_remote_copy(
            src_ref=dbuf.at[p, pl.ds(height - R, R), cols],
            dst_ref=up.at[p, :, cols],
            send_sem=down_send.at[p],
            recv_sem=up_recv.at[p, b],
            device_id={"trow": me + 1},
            device_id_type=MESH,
        )

    def send_halo(p, b):
        cols = pl.ds(pl.multiple_of(b * CB, CB), CB)

        @pl.when(has_up)
        def _():
            up_copy(p, cols, b).start()

        @pl.when(has_down)
        def _():
            down_copy(p, cols, b).start()

    def wait_halo(p, b):
        cols = pl.ds(pl.multiple_of(b * CB, CB), CB)

        @pl.when(has_up)
        def _():
            down_copy(p, cols, b).wait_recv()

        @pl.when(has_down)
        def _():
            up_copy(p, cols, b).wait_recv()

    def add_cell(b, value):
        part = jnp.sum(value.reshape(height // 8, 8, CB), axis=0)
        accs[b * CB // F] += part[:, :LANES] + part[:, LANES:]

    def keep(p, b, value):
        cols = pl.ds(pl.multiple_of(b * CB, CB), CB)
        dbuf[p, :, cols] = value
        high, low = split(value)
        dh[p % 2, :, cols] = high
        dl[p % 2, :, cols] = low

    def make_target(b, carry):
        cols = pl.ds(pl.multiple_of(b * CB, CB), CB)
        for hbm, buf, k in ((cov_hbm, cov, 0), (dose_hbm, dose, 1)):
            pltpu.make_async_copy(hbm.at[:, cols], buf.at[:, cols], load_sem.at[k, b]).wait()
        target = jnp.where(cov[:, cols] == 1, dose[:, cols], 0.0)
        keep(0, b, target)
        add_cell(b, target)
        send_halo(0, b)
        return carry

    lax.fori_loop(0, blocks, make_target, 0)
    for copy in consts:
        copy.wait()

    lane = lax.broadcasted_iota(jnp.int32, (1, LANES), 1) // group

    def coarse(o):
        row = jnp.zeros((1, LANES), jnp.float32)
        for e in range(cells):
            weight = jnp.zeros((1, LANES), jnp.float32)
            for c in range(cells):
                weight = jnp.where(lane == c, float(back_weight(float(e - c)) / (F * F)), weight)
            row = row + jnp.sum(accs[e], axis=(0, 1), keepdims=True) * weight
        row_out[o] = row
        first = pltpu.make_async_remote_copy(
            src_ref=row_out.at[o],
            dst_ref=row_in.at[o],
            send_sem=a_send.at[o],
            recv_sem=a_recv.at[o],
            device_id={"trow": partner},
            device_id_type=MESH,
        )
        first.start()
        first.wait_recv()
        yrows[o, y] = row + row_in[o]
        for d in range(1, ny):
            pltpu.make_async_remote_copy(
                src_ref=yrows.at[o, y],
                dst_ref=yrows.at[o, y],
                send_sem=y_send.at[o],
                recv_sem=y_recv.at[o],
                device_id={"trow": device((y + d) % ny, x, core)},
                device_id_type=MESH,
            ).start()
        several_y(o).wait_recv()

        def toward(xx):
            total = jnp.zeros((1, LANES), jnp.float32)
            for yy in range(ny):
                total = total + gtab[(y - yy) * nx + xx - x + (nx * ny - 1)] * yrows[o, yy]
            return total

        def send_x(d, k):
            xx = (x + d) % nx
            xout[o, k] = toward(xx)
            for cc in range(2):
                pltpu.make_async_remote_copy(
                    src_ref=xout.at[o, k],
                    dst_ref=xrows.at[o, x],
                    send_sem=x_send.at[o],
                    recv_sem=x_recv.at[o],
                    device_id={"trow": device(y, xx, cc)},
                    device_id_type=MESH,
                ).start()

        @pl.when(core == 0)
        def _():
            for d in range(fwd, 0, -1):
                send_x(d, d - 1)

        @pl.when(core == 1)
        def _():
            for d in range(bwd, 0, -1):
                send_x(nx - d, d - 1)

        xrows[o, x] = toward(x)
        several_x(o, nx - 1).wait_recv()
        total = jnp.zeros((1, LANES), jnp.float32)
        for xx in range(nx):
            total = total + xrows[o, xx]
        total = total * backscatter_ratio
        for c in range(cells):
            spread[c] = jnp.broadcast_to(total[:, c * group : c * group + 1], (8, LANES))

    def several_y(o):
        return pltpu.make_async_remote_copy(
            src_ref=yrows.at[o, pl.ds(0, ny - 1)],
            dst_ref=yrows.at[o, pl.ds(0, ny - 1)],
            send_sem=y_send.at[o],
            recv_sem=y_recv.at[o],
            device_id={"trow": partner},
            device_id_type=MESH,
        )

    def several_x(o, count):
        return pltpu.make_async_remote_copy(
            src_ref=xrows.at[o, pl.ds(0, count)],
            dst_ref=xrows.at[o, pl.ds(0, count)],
            send_sem=x_send.at[o],
            recv_sem=x_recv.at[o],
            device_id={"trow": partner},
            device_id_type=MESH,
        )

    def vertical(p, b):
        cols = pl.ds(pl.multiple_of(b * CB, CB), CB)
        wait_halo(p, b)
        halo = jnp.concatenate([up[p, :, cols], down[p, :, cols]], axis=0)
        halo_high, halo_low = split(halo)
        own_high, own_low = dh[p % 2, :, cols], dl[p % 2, :, cols]
        value = (
            dot(ah[:, :height], own_high)
            + dot(ah[:, height:], halo_high)
            + dot(ah[:, :height], own_low)
            + dot(ah[:, height:], halo_low)
            + dot(al[:, :height], own_high)
            + dot(al[:, height:], halo_high)
        )
        high, low = split(value)
        inside = pl.ds(pl.multiple_of(b * CB + R, R), CB)
        vh[:, inside] = high
        vl[:, inside] = low

    def finish(p, b):
        cols = pl.ds(pl.multiple_of(b * CB, CB), CB)
        framed = pl.ds(pl.multiple_of(b * CB, CB), CB + 2 * R)
        high, low = vh[:, framed], vl[:, framed]
        value = dot(high, bh[...]) + dot(low, bh[...]) + dot(high, bl[...])
        far = spread[b * CB // F][0:1]
        exposure = value + jnp.concatenate([far] * (CB // LANES), axis=1)
        dosage = dbuf[p, :, cols] * dbuf[0, :, cols] / exposure
        if p < PASSES - 1:
            keep(p + 1, b, dosage)
            if (p + 1) % INNER == 0:
                add_cell(b, dosage)
            send_halo(p + 1, b)
        else:
            dout[:, cols] = dosage
            eout[:, cols] = exposure
            pltpu.make_async_copy(dout.at[:, cols], dout_hbm.at[:, cols], out_sem.at[0]).start()
            pltpu.make_async_copy(eout.at[:, cols], eout_hbm.at[:, cols], out_sem.at[1]).start()

    for p in range(PASSES):
        if p % INNER == 0:
            coarse(p // INNER)
            accs[...] = jnp.zeros_like(accs)
        vertical(p, 0)

        def step(b, carry, p=p):
            vertical(p, b)
            finish(p, b - 1)
            return carry

        lax.fori_loop(1, blocks, step, 0)
        finish(p, blocks - 1)

    every = pl.ds(0, width)
    for p in range(PASSES):

        @pl.when(has_up)
        def _(p=p):
            up_copy(p, every, 0).wait_send()

        @pl.when(has_down)
        def _(p=p):
            down_copy(p, every, 0).wait_send()

    for o in range(OUTER):
        pltpu.make_async_remote_copy(
            src_ref=row_out.at[o],
            dst_ref=row_in.at[o],
            send_sem=a_send.at[o],
            recv_sem=a_recv.at[o],
            device_id={"trow": partner},
            device_id_type=MESH,
        ).wait_send()
        several_y(o).wait_send()

        @pl.when(core == 0)
        def _(o=o):
            several_x(o, 2 * fwd).wait_send()

        if bwd:

            @pl.when(core == 1)
            def _(o=o):
                several_x(o, 2 * bwd).wait_send()

    pltpu.make_async_copy(dout, dout_hbm, out_sem.at[0]).wait()
    pltpu.make_async_copy(eout, eout_hbm, out_sem.at[1]).wait()


def solution(mesh):
    n = mesh.shape["trow"]
    chips = n // 2
    nx = max(d for d in range(1, math.isqrt(chips) + 1) if chips % d == 0)
    ny = chips // nx

    def per_device(coverage, dose_level):
        height, width = coverage.shape
        blocks, cells = width // CB, width // F
        assert 2 * height == F and width % F == 0 and height == 2 * R
        ah, al = two_parts(vertical_matrix(height))
        bh, bl = two_parts(horizontal_matrix())
        steps = np.arange(2 * chips, dtype=np.float64) - (chips - 1)
        gtab = jnp.asarray(
            np.broadcast_to(back_weight(steps)[:, None, None], (2 * chips, 1, LANES)), jnp.float32
        )
        f32, bf16 = jnp.float32, jnp.bfloat16
        dma = pltpu.SemaphoreType.DMA
        shape = jax.ShapeDtypeStruct((height, width), f32)
        return pl.pallas_call(
            functools.partial(kernel, n, nx, ny),
            out_shape=(shape, shape),
            in_specs=[pl.BlockSpec(memory_space=pl.ANY)] * 7,
            out_specs=(pl.BlockSpec(memory_space=pl.ANY),) * 2,
            scratch_shapes=[
                pltpu.VMEM((height, width), jnp.int32),
                pltpu.VMEM((height, width), f32),
                pltpu.VMEM(ah.shape, bf16),
                pltpu.VMEM(al.shape, bf16),
                pltpu.VMEM(bh.shape, bf16),
                pltpu.VMEM(bl.shape, bf16),
                pltpu.VMEM(gtab.shape, f32),
                pltpu.VMEM((PASSES, height, width), f32),
                pltpu.VMEM((2, height, width), bf16),
                pltpu.VMEM((2, height, width), bf16),
                pltpu.VMEM((PASSES, R, width), f32),
                pltpu.VMEM((PASSES, R, width), f32),
                pltpu.VMEM((height, width + 2 * R), bf16),
                pltpu.VMEM((height, width + 2 * R), bf16),
                pltpu.VMEM((height, width), f32),
                pltpu.VMEM((height, width), f32),
                pltpu.VMEM((cells, 8, LANES), f32),
                pltpu.VMEM((cells, 8, LANES), f32),
                pltpu.VMEM((OUTER, 1, LANES), f32),
                pltpu.VMEM((OUTER, 1, LANES), f32),
                pltpu.VMEM((OUTER, ny, 1, LANES), f32),
                pltpu.VMEM((OUTER, nx, 1, LANES), f32),
                pltpu.VMEM((OUTER, 2 * nx, 1, LANES), f32),
                dma((2, blocks)),
                dma((5,)),
                dma((2,)),
                dma((PASSES,)),
                dma((PASSES,)),
                dma((PASSES, blocks)),
                dma((PASSES, blocks)),
                dma((OUTER,)),
                dma((OUTER,)),
                dma((OUTER,)),
                dma((OUTER,)),
                dma((OUTER,)),
                dma((OUTER,)),
            ],
            compiler_params=pltpu.CompilerParams(
                collective_id=0, has_side_effects=True, vmem_limit_bytes=60 * 2**20
            ),
            name="dose",
        )(coverage, dose_level, ah, al, bh, bl, gtab)

    spec = P(("win", "trow"), None)
    return jax.shard_map(
        per_device, mesh=mesh, in_specs=(spec, spec), out_specs=(spec, spec), check_vma=False
    )
```

time: 281 us -> 88.7 us (0.32)
  the two profiles are of different devices: /device:TPU:513 before, /device:TPU:522 now
where the time goes in v1:
time: 88.7 us; the launch traced here: 88.6 us
  Pallas kernels  83.4 us (94%)
  local copies, waits for them, and re-layouts  4.61 us (5%)
    pallas_call x1, Pallas kernels, per_device(): pl.pallas_call(functools.partial(kernel, n, nx, ny), out_shape=(shape, sh...  83.4 us
    unnamed x4, local copies, waits for them, and re-layouts  4.61 us

profile of v1, /device:TPU:522, one launch (start us, length us, event | category | flops | bytes accessed | tf_op | source)
XLA Modules:
  0.0 88.6 jit_solution(6698376265869648897)
XLA Ops:
  0.6 83.4 %dose.1 = (f32[256,2048]{1,0:T(8,128)}, f32[256,2048]{1,0:T(8,128)}) custom-call(s32[256,2048]{1,0:T(8,128)} %cov_hbm.1, f32[256,2048]{1,0:T(8,128)} %dose_hbm.1, bf16[256,512]{1,0:T(8,128)(2,1)} %constant.9.ah_hbm, bf16[256,512]{1,0:T(8,128)(2,1)} %constant.12.al_hbm, bf16[512,256]{1,0:T(8,128)(2,1)} %constant.13.bh_hbm, bf16[512,256]{1,0:T(8,128)(2,1)} %constant.16.bl_hbm, ...), custom_call_target="tpu_custom_call" | custom-call | tf_op jit(solution)/shard_map/dose/pallas_call | solution.py:427
  84.0 0.0 copy-start
  84.0 3.3 %copy.9 = f32[256,2048]{1,0:T(8,128)} copy(f32[256,2048]{1,0:T(8,128)} %get-tuple-element.4) | data formatting | bytes 4194304
  87.3 0.0 copy-done
  87.3 1.3 %copy.10 = f32[256,2048]{1,0:T(8,128)} copy(f32[256,2048]{1,0:T(8,128)S(1)} %copy-done) | data formatting | bytes 4194304
Async XLA Ops:
  84.0 3.3 %copy-start = (f32[256,2048]{1,0:T(8,128)S(1)}, f32[256,2048]{1,0:T(8,128)}, u32[]{:S(2)}) copy-start(f32[256,2048]{1,0:T(8,128)} %get-tuple-element.5) | copy-start | bytes 6291460

commit v2 on v1

v2 whole, which is shorter than its diff:
```python
import functools
import math

import jax
import jax.numpy as jnp
import numpy as np
from jax import lax
from jax.experimental import pallas as pl
from jax.experimental.pallas import tpu as pltpu
from jax.sharding import PartitionSpec as P

R = 128
F = 512
SIG_FWD = 5
SIG_MID = 50
SIG_BACK = 3000
OUTER = 2
INNER = 2
PASSES = OUTER * INNER
CB = 256
LANES = 128
backscatter_ratio = 0.7
MESH = pl.DeviceIdType.MESH


def raw_profile(offset):
    first = 0.5 * np.exp(-offset * offset / (2.0 * SIG_FWD**2)) / SIG_FWD
    second = 0.5 * np.exp(-offset * offset / (2.0 * SIG_MID**2)) / SIG_MID
    return first + second


def short_weight(offset):
    normal = np.sum(raw_profile(np.arange(-R, R + 1, dtype=np.float64)))
    return np.where(np.abs(offset) <= R, raw_profile(offset) / normal, 0.0)


def back_weight(offset):
    spacing = offset * F
    return (
        F
        * np.exp(-spacing * spacing / (2.0 * SIG_BACK**2))
        / (math.sqrt(2.0 * math.pi) * SIG_BACK)
    )


def two_parts(matrix):
    whole = jnp.asarray(matrix, jnp.float32)
    high = whole.astype(jnp.bfloat16)
    low = (whole - high.astype(jnp.float32)).astype(jnp.bfloat16)
    return high, low


def vertical_matrix(rows):
    out = np.arange(rows, dtype=np.float64)[:, None]
    own = np.arange(rows, dtype=np.float64)
    above = np.arange(-R, 0, dtype=np.float64)
    below = np.arange(rows, rows + R, dtype=np.float64)
    return short_weight(out - np.concatenate([own, above, below])[None, :])


def horizontal_matrix():
    inner = np.arange(CB + 2 * R, dtype=np.float64)[:, None]
    outer = np.arange(CB, dtype=np.float64)[None, :]
    return short_weight(inner - R - outer)


def split(value):
    high = value.astype(jnp.bfloat16)
    low = (value - high.astype(jnp.float32)).astype(jnp.bfloat16)
    return high, low


def dot(left, right):
    return jnp.dot(left, right, preferred_element_type=jnp.float32)


def kernel(
    n, nx, ny,
    cov_hbm, dose_hbm, ah_hbm, al_hbm, bh_hbm, bl_hbm, gtab_hbm,
    dout, eout,
    cov, dose, ah, al, bh, bl, gtab,
    field, middle, own_sum, up, down, vh, vl,
    accs, spread, row_out, row_in, yrows, xout, xrows,
    load_sem, const_sem,
    up_send, down_send, up_recv, down_recv,
    a_send, a_recv, y_send, y_recv, x_send, x_recv,
):
    height, width = cov.shape
    blocks = width // CB
    cells = width // F
    group = LANES // cells
    me = lax.axis_index("trow")
    chip, core = me // 2, me % 2
    y, x = chip // nx, chip % nx
    partner = me + 1 - 2 * core
    has_up, has_down = me > 0, me < n - 1
    fwd, bwd = nx // 2, (nx - 1) // 2

    def device(yy, xx, cc):
        return (yy * nx + xx) * 2 + cc

    def load(b):
        cols = pl.ds(b * CB, CB)
        return (
            pltpu.make_async_copy(cov_hbm.at[:, cols], cov.at[:, cols], load_sem.at[0, b]),
            pltpu.make_async_copy(dose_hbm.at[:, cols], dose.at[:, cols], load_sem.at[1, b]),
        )

    for b in range(blocks):
        for copy in load(b):
            copy.start()
    consts = [
        pltpu.make_async_copy(source, target, const_sem.at[k])
        for k, (source, target) in enumerate(
            [(ah_hbm, ah), (al_hbm, al), (bh_hbm, bh), (bl_hbm, bl), (gtab_hbm, gtab)]
        )
    ]
    for copy in consts:
        copy.start()

    barrier = pltpu.get_barrier_semaphore()

    def greet(other):
        pl.semaphore_signal(barrier, inc=1, device_id={"trow": other}, device_id_type=MESH)

    @pl.when(has_up)
    def _():
        greet(me - 1)

    @pl.when(has_down)
    def _():
        greet(me + 1)

    for d in range(1, ny):
        greet(device((y + d) % ny, x, core))
    for d in range(1, fwd + 1):
        greet(device(y, (x + nx - d) % nx, 0))
    for d in range(1, bwd + 1):
        greet(device(y, (x + d) % nx, 1))

    accs[...] = jnp.zeros_like(accs)
    def up_copy(p, cols, b):
        return pltpu.make_async_remote_copy(
            src_ref=field.at[p, pl.ds(0, R), cols],
            dst_ref=down.at[p, :, cols],
            send_sem=up_send.at[p],
            recv_sem=down_recv.at[p, b],
            device_id={"trow": me - 1},
            device_id_type=MESH,
        )

    def down_copy(p, cols, b):
        return pltpu.make_async_remote_copy(
            src_ref=field.at[p, pl.ds(height - R, R), cols],
            dst_ref=up.at[p, :, cols],
            send_sem=down_send.at[p],
            recv_sem=up_recv.at[p, b],
            device_id={"trow": me + 1},
            device_id_type=MESH,
        )

    def send_halo(p, b):
        cols = pl.ds(pl.multiple_of(b * CB, CB), CB)

        @pl.when(has_up)
        def _():
            up_copy(p, cols, b).start()

        @pl.when(has_down)
        def _():
            down_copy(p, cols, b).start()

    def wait_halo(p, b):
        cols = pl.ds(pl.multiple_of(b * CB, CB), CB)

        @pl.when(has_up)
        def _():
            down_copy(p, cols, b).wait_recv()

        @pl.when(has_down)
        def _():
            up_copy(p, cols, b).wait_recv()

    def add_cell(b, value):
        part = jnp.sum(value.reshape(value.shape[0] // 8, 8, CB), axis=0)
        accs[b * CB // F] += part[:, :LANES] + part[:, LANES:]

    chunk = 64

    def make_target(b, carry):
        cols = pl.ds(pl.multiple_of(b * CB, CB), CB)
        for hbm, buf, k in ((cov_hbm, cov, 0), (dose_hbm, dose, 1)):
            pltpu.make_async_copy(hbm.at[:, cols], buf.at[:, cols], load_sem.at[k, b]).wait()
        for r in range(0, height, chunk):
            rows = pl.ds(r, chunk)
            target = jnp.where(cov[rows, cols] == 1, dose[rows, cols], 0.0)
            field[0, rows, cols] = target
            add_cell(b, target)
        return carry

    lax.fori_loop(0, blocks, make_target, 0)
    pl.semaphore_wait(
        barrier,
        has_up.astype(jnp.int32)
        + has_down.astype(jnp.int32)
        + (ny - 1)
        + 2 * jnp.where(core == 0, fwd, bwd),
    )

    lane = lax.broadcasted_iota(jnp.int32, (1, LANES), 1) // group

    def coarse_start(o):
        row = jnp.zeros((1, LANES), jnp.float32)
        for e in range(cells):
            weight = jnp.zeros((1, LANES), jnp.float32)
            for c in range(cells):
                weight = jnp.where(lane == c, float(back_weight(float(e - c)) / (F * F)), weight)
            row = row + jnp.sum(accs[e], axis=(0, 1), keepdims=True) * weight
        row_out[o] = row
        pair(o).start()
        accs[...] = jnp.zeros_like(accs)

    def coarse_y(o):
        pair(o).wait_recv()
        yrows[o, y] = row_out[o] + row_in[o]
        for d in range(1, ny):
            pltpu.make_async_remote_copy(
                src_ref=yrows.at[o, y],
                dst_ref=yrows.at[o, y],
                send_sem=y_send.at[o],
                recv_sem=y_recv.at[o],
                device_id={"trow": device((y + d) % ny, x, core)},
                device_id_type=MESH,
            ).start()

    def coarse_x(o):
        several_y(o).wait_recv()

        def toward(xx, shift):
            total = jnp.zeros((1, LANES), jnp.float32)
            for yy in range(ny):
                total = total + gtab[(y - yy) * nx + xx - x + shift + nx * ny] * yrows[o, yy]
            return total

        def send_x(d, k):
            xx = (x + d) % nx
            here = toward(xx, 0)
            for cc in range(2):
                xout[o, k, cc, 0] = here
                xout[o, k, cc, 1] = toward(xx, 2 * cc - 1)
            for cc in range(2):
                pltpu.make_async_remote_copy(
                    src_ref=xout.at[o, k, cc],
                    dst_ref=xrows.at[o, x],
                    send_sem=x_send.at[o],
                    recv_sem=x_recv.at[o],
                    device_id={"trow": device(y, xx, cc)},
                    device_id_type=MESH,
                ).start()

        @pl.when(core == 0)
        def _():
            for d in range(fwd, 0, -1):
                send_x(d, d - 1)

        @pl.when(core == 1)
        def _():
            for d in range(bwd, 0, -1):
                send_x(nx - d, d - 1)

        xrows[o, x, 0] = toward(x, 0)
        xrows[o, x, 1] = toward(x, 2 * core - 1)

    def coarse_end(o):
        several_x(o, nx - 1).wait_recv()
        for k in range(2):
            total = jnp.zeros((1, LANES), jnp.float32)
            for xx in range(nx):
                total = total + xrows[o, xx, k]
            total = total * backscatter_ratio
            for c in range(cells):
                spread[k, c] = jnp.broadcast_to(total[:, c * group : c * group + 1], (8, LANES))

    def pair(o):
        return pltpu.make_async_remote_copy(
            src_ref=row_out.at[o],
            dst_ref=row_in.at[o],
            send_sem=a_send.at[o],
            recv_sem=a_recv.at[o],
            device_id={"trow": partner},
            device_id_type=MESH,
        )

    def several_y(o):
        return pltpu.make_async_remote_copy(
            src_ref=yrows.at[o, pl.ds(0, ny - 1)],
            dst_ref=yrows.at[o, pl.ds(0, ny - 1)],
            send_sem=y_send.at[o],
            recv_sem=y_recv.at[o],
            device_id={"trow": partner},
            device_id_type=MESH,
        )

    def several_x(o, count):
        return pltpu.make_async_remote_copy(
            src_ref=xrows.at[o, pl.ds(0, count)],
            dst_ref=xrows.at[o, pl.ds(0, count)],
            send_sem=x_send.at[o],
            recv_sem=x_recv.at[o],
            device_id={"trow": partner},
            device_id_type=MESH,
        )

    def columns(b):
        return pl.ds(pl.multiple_of(b * CB, CB), CB)

    def far(which, b):
        row = spread[which, b * CB // F]
        return jnp.concatenate([row] * (CB // LANES), axis=1)[0:1]

    def own_product(value):
        high, low = split(value)
        return (
            dot(ah[:, :height], high) + dot(ah[:, :height], low) + dot(al[:, :height], high)
        )

    def halo_product(above, below):
        high, low = split(jnp.concatenate([above, below], axis=0))
        return (
            dot(ah[:, height:], high) + dot(ah[:, height:], low) + dot(al[:, height:], high)
        )

    def store_vertical(b, value):
        high, low = split(value)
        inside = pl.ds(pl.multiple_of(b * CB + R, R), CB)
        vh[:, inside] = high
        vl[:, inside] = low

    def horizontal(b):
        framed = pl.ds(pl.multiple_of(b * CB, CB), CB + 2 * R)
        high, low = vh[:, framed], vl[:, framed]
        return dot(high, bh[...]) + dot(low, bh[...]) + dot(high, bl[...])

    def first_vertical(p, b):
        cols = columns(b)
        wait_halo(p, b)
        store_vertical(b, own_sum[:, cols] + halo_product(up[p, :, cols], down[p, :, cols]))

    def first_finish(p, b):
        field[p + 1, :, columns(b)] = horizontal(b)
        send_halo(p + 1, b)

    def second_vertical(p, b):
        cols = columns(b)
        wait_halo(p, b)
        here = far(0, b)
        for r in range(0, height, chunk):
            rows = pl.ds(r, chunk)
            middle[rows, cols] = (
                field[p - 1, rows, cols] * field[0, rows, cols] / (field[p, rows, cols] + here)
            )
        edge = []
        for halo, which in ((up, 1 - core), (down, core)):
            edge.append(halo[p - 1, :, cols] * halo[0, :, cols] / (halo[p, :, cols] + far(which, b)))
        store_vertical(b, own_product(middle[:, cols]) + halo_product(*edge))

    def second_finish(p, b):
        cols = columns(b)
        eout[:, cols] = horizontal(b)
        here = far(0, b)
        for r in range(0, height, chunk):
            rows = pl.ds(r, chunk)
            exposure = eout[rows, cols] + here
            dosage = middle[rows, cols] * field[0, rows, cols] / exposure
            if p < PASSES - 1:
                field[p + 1, rows, cols] = dosage
                add_cell(b, dosage)
            else:
                dout[rows, cols] = dosage
                eout[rows, cols] = exposure
        if p < PASSES - 1:
            send_halo(p + 1, b)

    def run(p, vertical, finish):
        vertical(p, 0)

        def step(b, carry):
            vertical(p, b)
            finish(p, b - 1)
            return carry

        lax.fori_loop(1, blocks, step, 0)
        finish(p, blocks - 1)

    coarse_start(0)

    def send_target(b, carry):
        send_halo(0, b)
        return carry

    lax.fori_loop(0, blocks, send_target, 0)
    zero_pad = jnp.zeros((height, R), jnp.bfloat16)
    for part in (vh, vl):
        part[:, 0:R] = zero_pad
        part[:, R + width : R + width + R] = zero_pad

    @pl.when(me == 0)
    def _():
        up[...] = jnp.zeros_like(up)

    @pl.when(me == n - 1)
    def _():
        down[...] = jnp.zeros_like(down)

    for copy in consts:
        copy.wait()

    for o in range(OUTER):
        p = INNER * o
        if o:
            coarse_start(o)
        coarse_y(o)

        def own(b, carry, p=p):
            own_sum[:, columns(b)] = own_product(field[p, :, columns(b)])
            return carry

        lax.fori_loop(0, blocks, own, 0)
        coarse_x(o)
        run(p, first_vertical, first_finish)
        coarse_end(o)
        run(p + 1, second_vertical, second_finish)

    every = pl.ds(0, width)
    for p in range(PASSES):

        @pl.when(has_up)
        def _(p=p):
            up_copy(p, every, 0).wait_send()

        @pl.when(has_down)
        def _(p=p):
            down_copy(p, every, 0).wait_send()

    for o in range(OUTER):
        pair(o).wait_send()
        several_y(o).wait_send()

        @pl.when(core == 0)
        def _(o=o):
            several_x(o, 2 * fwd).wait_send()

        if bwd:

            @pl.when(core == 1)
            def _(o=o):
                several_x(o, 2 * bwd).wait_send()


def solution(mesh):
    n = mesh.shape["trow"]
    chips = n // 2
    nx = max(d for d in range(1, math.isqrt(chips) + 1) if chips % d == 0)
    ny = chips // nx

    def per_device(coverage, dose_level):
        height, width = coverage.shape
        blocks, cells = width // CB, width // F
        assert 2 * height == F and width % F == 0 and height == 2 * R
        ah, al = two_parts(vertical_matrix(height))
        bh, bl = two_parts(horizontal_matrix())
        steps = np.arange(2 * chips + 1, dtype=np.float64) - chips
        gtab = jnp.asarray(
            np.broadcast_to(back_weight(steps)[:, None, None], (2 * chips + 1, 1, LANES)), jnp.float32
        )
        f32, bf16 = jnp.float32, jnp.bfloat16
        dma = pltpu.SemaphoreType.DMA
        dosage, exposure = pl.pallas_call(
            functools.partial(kernel, n, nx, ny),
            out_shape=(pltpu.VMEM((height, width), f32), pltpu.VMEM((height, width), f32)),
            in_specs=[pl.BlockSpec(memory_space=pl.ANY)] * 7,
            out_specs=(pl.BlockSpec(memory_space=pltpu.VMEM),) * 2,
            scratch_shapes=[
                pltpu.VMEM((height, width), jnp.int32),
                pltpu.VMEM((height, width), f32),
                pltpu.VMEM(ah.shape, bf16),
                pltpu.VMEM(al.shape, bf16),
                pltpu.VMEM(bh.shape, bf16),
                pltpu.VMEM(bl.shape, bf16),
                pltpu.VMEM(gtab.shape, f32),
                pltpu.VMEM((PASSES, height, width), f32),
                pltpu.VMEM((height, width), f32),
                pltpu.VMEM((height, width), f32),
                pltpu.VMEM((PASSES, R, width), f32),
                pltpu.VMEM((PASSES, R, width), f32),
                pltpu.VMEM((height, width + 2 * R), bf16),
                pltpu.VMEM((height, width + 2 * R), bf16),
                pltpu.VMEM((cells, 8, LANES), f32),
                pltpu.VMEM((2, cells, 8, LANES), f32),
                pltpu.VMEM((OUTER, 1, LANES), f32),
                pltpu.VMEM((OUTER, 1, LANES), f32),
                pltpu.VMEM((OUTER, ny, 1, LANES), f32),
                pltpu.VMEM((OUTER, nx, 2, 2, 1, LANES), f32),
                pltpu.VMEM((OUTER, 2 * nx, 2, 1, LANES), f32),
                dma((2, blocks)),
                dma((5,)),
                dma((PASSES,)),
                dma((PASSES,)),
                dma((PASSES, blocks)),
                dma((PASSES, blocks)),
                dma((OUTER,)),
                dma((OUTER,)),
                dma((OUTER,)),
                dma((OUTER,)),
                dma((OUTER,)),
                dma((OUTER,)),
            ],
            compiler_params=pltpu.CompilerParams(
                collective_id=0, has_side_effects=True, vmem_limit_bytes=(59 * 2 + 1) * 2**19
            ),
            name="dose",
        )(coverage, dose_level, ah, al, bh, bl, gtab)
        return dosage, exposure

    spec = P(("win", "trow"), None)
    return jax.shard_map(
        per_device, mesh=mesh, in_specs=(spec, spec), out_specs=(spec, spec), check_vma=False
    )
```

time: 88.7 us -> 74.8 us (0.84)
  the two profiles are of different devices: /device:TPU:522 before, /device:TPU:519 now
where the time goes in v2:
time: 74.8 us; the launch traced here: 74.7 us
  Pallas kernels  71.4 us (95%)
  local copies, waits for them, and re-layouts  2.64 us (4%)
    pallas_call x1, Pallas kernels, per_device(): pl.pallas_call(functools.partial(kernel, n, nx, ny), out_shape=(pltpu.VME...  71.4 us
    unnamed x2, local copies, waits for them, and re-layouts  2.64 us

profile of v2, /device:TPU:519, one launch (start us, length us, event | category | flops | bytes accessed | tf_op | source)
XLA Modules:
  0.0 74.7 jit_solution(6470266039403855623)
XLA Ops:
  0.6 71.4 %dose.1 = (f32[256,2048]{1,0:T(8,128)S(1)}, f32[256,2048]{1,0:T(8,128)S(1)}) custom-call(s32[256,2048]{1,0:T(8,128)} %cov_hbm.1, f32[256,2048]{1,0:T(8,128)} %dose_hbm.1, bf16[256,512]{1,0:T(8,128)(2,1)} %constant.9.ah_hbm, bf16[256,512]{1,0:T(8,128)(2,1)} %constant.12.al_hbm, bf16[512,256]{1,0:T(8,128)(2,1)} %constant.13.bh_hbm, ...), custom_call_target="tpu_custom_call" | custom-call | tf_op jit(solution)/shard_map/dose/pallas_call | solution.py:478
  72.1 1.3 %copy.9 = f32[256,2048]{1,0:T(8,128)} copy(f32[256,2048]{1,0:T(8,128)S(1)} %get-tuple-element.2) | data formatting | bytes 4194304
  73.4 1.3 %copy.10 = f32[256,2048]{1,0:T(8,128)} copy(f32[256,2048]{1,0:T(8,128)S(1)} %get-tuple-element.3) | data formatting | bytes 4194304

commit v3 on v2

--- a/solution.py
+++ b/solution.py
@@ -94,7 +94,7 @@
     y, x = chip // nx, chip % nx
     partner = me + 1 - 2 * core
     has_up, has_down = me > 0, me < n - 1
-    fwd, bwd = nx // 2, (nx - 1) // 2
+    fwd, bwd = (nx - 1) // 2, nx // 2
 
     def device(yy, xx, cc):
         return (yy * nx + xx) * 2 + cc
@@ -381,16 +381,19 @@
         if p < PASSES - 1:
             send_halo(p + 1, b)
 
-    def run(p, vertical, finish):
-        vertical(p, 0)
+    def run(p, vertical, finish, first, last):
+        if first == 0:
+            vertical(p, 0)
+            first = 1
 
         def step(b, carry):
             vertical(p, b)
             finish(p, b - 1)
             return carry
 
-        lax.fori_loop(1, blocks, step, 0)
-        finish(p, blocks - 1)
+        lax.fori_loop(first, last, step, 0)
+        if last == blocks:
+            finish(p, blocks - 1)
 
     coarse_start(0)
 
@@ -426,10 +429,13 @@
             return carry
 
         lax.fori_loop(0, blocks, own, 0)
+        early = 0
+        if early:
+            run(p, first_vertical, first_finish, 0, early)
         coarse_x(o)
-        run(p, first_vertical, first_finish)
+        run(p, first_vertical, first_finish, early, blocks)
         coarse_end(o)
-        run(p + 1, second_vertical, second_finish)
+        run(p + 1, second_vertical, second_finish, 0, blocks)
 
     every = pl.ds(0, width)
     for p in range(PASSES):
@@ -455,6 +461,17 @@
             @pl.when(core == 1)
             def _(o=o):
                 several_x(o, 2 * bwd).wait_send()
+
+
+def write_out(dout, eout, dout_hbm, eout_hbm, sems):
+    copies = [
+        pltpu.make_async_copy(dout, dout_hbm, sems.at[0]),
+        pltpu.make_async_copy(eout, eout_hbm, sems.at[1]),
+    ]
+    for copy in copies:
+        copy.start()
+    for copy in copies:
+        copy.wait()
 
 
 def solution(mesh):
@@ -520,7 +537,16 @@
             ),
             name="dose",
         )(coverage, dose_level, ah, al, bh, bl, gtab)
-        return dosage, exposure
+        shape = jax.ShapeDtypeStruct((height, width), f32)
+        return pl.pallas_call(
+            write_out,
+            out_shape=(shape, shape),
+            in_specs=[pl.BlockSpec(memory_space=pl.ANY)] * 2,
+            out_specs=(pl.BlockSpec(memory_space=pl.ANY),) * 2,
+            scratch_shapes=[dma((2,))],
+            compiler_params=pltpu.CompilerParams(vmem_limit_bytes=2**20),
+            name="write_out",
+        )(dosage, exposure)
 
     spec = P(("win", "trow"), None)
     return jax.shard_map(

time: 74.8 us -> 74.3 us (level)
  the two profiles are of different devices: /device:TPU:519 before, /device:TPU:513 now
where the time goes in v3:
time: 74.3 us; the launch traced here: 74.2 us
  Pallas kernels  73.5 us (99%)
    pallas_call x1, Pallas kernels, per_device(): pl.pallas_call(functools.partial(kernel, n, nx, ny), out_shape=(pltpu.VME...  71.5 us
    pallas_call x1, Pallas kernels, per_device(): pl.pallas_call(write_out, out_shape=(shape, shape), in_specs=[pl.BlockSpe...  2.03 us

profile of v3, /device:TPU:513, one launch (start us, length us, event | category | flops | bytes accessed | tf_op | source)
XLA Modules:
  0.0 74.2 jit_solution(15922625279013392865)
XLA Ops:
  0.6 71.5 %dose.1 = (f32[256,2048]{1,0:T(8,128)S(1)}, f32[256,2048]{1,0:T(8,128)S(1)}) custom-call(s32[256,2048]{1,0:T(8,128)} %cov_hbm.1, f32[256,2048]{1,0:T(8,128)} %dose_hbm.1, bf16[256,512]{1,0:T(8,128)(2,1)} %constant.9.ah_hbm, bf16[256,512]{1,0:T(8,128)(2,1)} %constant.12.al_hbm, bf16[512,256]{1,0:T(8,128)(2,1)} %constant.13.bh_hbm, ...), custom_call_target="tpu_custom_call" | custom-call | tf_op jit(solution)/shard_map/dose/pallas_call | solution.py:495
  72.1 2.0 %write_out.1 = (f32[256,2048]{1,0:T(8,128)}, f32[256,2048]{1,0:T(8,128)}) custom-call(f32[256,2048]{1,0:T(8,128)S(1)} %get-tuple-element.4.dout, f32[256,2048]{1,0:T(8,128)S(1)} %get-tuple-element.5.eout), custom_call_target="tpu_custom_call" | custom-call | tf_op jit(solution)/shard_map/write_out/pallas_call | solution.py:541
